TPU v7x, 8 devices: a whole 2x2x1 slice. The times are simulated.
8 devices in a mesh: data: 1 (over z), pp: 2 (over y), ep: 4 (over x, core).
Axes of the slice: x: 2, y: 2, z: 1, core: 2. Of those that a mesh axis runs over, the one named last changes fastest.
Arguments:
- O: bfloat16 [2, 8, 8, 640, 4096], P(('data', 'pp'), None, 'ep')
- idx: int32 [2, 8, 4, 512, 2], P(('data', 'pp'), None, 'ep')
- slot: int32 [2, 8, 4, 512, 2], P(('data', 'pp'), None, 'ep')
- g: float32 [2, 8, 4, 512, 2], P(('data', 'pp'), None, 'ep')
- H: bfloat16 [2, 8, 4, 512, 4096], P(('data', 'pp'), None, 'ep')
- w: float32 [2, 4096], P('pp')
- Wq: bfloat16 [2, 4096, 32, 128], P('pp')
- Wk: bfloat16 [2, 4096, 32, 128], P('pp')
- Wv: bfloat16 [2, 4096, 32, 128], P('pp')
- Wo: bfloat16 [2, 32, 128, 4096], P('pp')
Outputs:
- output: bfloat16 [2, 8, 4, 512, 4096], P(('data', 'pp'), None, 'ep')
All inputs are finite; a program needn't handle non-finite values.
Results may differ from a plain program's by a relative error of at most 0.00686826.
Values are sent between devices in bfloat16 or wider.
A program may use at most 1.25 GiB of HBM per device.

v0:
```python
import functools
import math

import jax
import jax.numpy as jnp
from jax import lax
from jax.experimental import pallas as pl
from jax.experimental.pallas import tpu as pltpu
from jax.sharding import PartitionSpec as P


EPS = 1e-6
HD = 128
F32 = jnp.float32
BF16 = jnp.bfloat16
VMEM_LIMIT = 63 * 1024 * 1024
ANY = pl.BlockSpec(memory_space=pl.ANY)
TOK = jax.ShapeDtypeStruct((8, 128), F32)


def cost(flops):
    return pl.CostEstimate(flops=int(flops), bytes_accessed=int(flops) // 256, transcendentals=0)


def slice_kernel(rows_ref, tok, o_ref, out_ref, tok_out):
    out_ref[...] = o_ref[...].reshape(out_ref.shape)


def slice_rows(rows, tok, o, m0, nm, cg):
    _, ne, _, d = o.shape
    n_own = rows.shape[0]
    return pl.pallas_call(
        slice_kernel,
        grid_spec=pltpu.PrefetchScalarGridSpec(
            num_scalar_prefetch=1,
            grid=(nm, n_own),
            in_specs=[ANY, pl.BlockSpec((1, ne, cg, d), lambda m, a, r: (m0 + m, 0, r[a], 0))],
            out_specs=[pl.BlockSpec((1, 1, ne, cg, d), lambda m, a, r: (m, a, 0, 0, 0)), ANY],
        ),
        out_shape=[jax.ShapeDtypeStruct((nm, n_own, ne, cg, d), o.dtype), TOK],
        input_output_aliases={1: 1},
        compiler_params=pltpu.CompilerParams(vmem_limit_bytes=VMEM_LIMIT),
        cost_estimate=cost(nm * 2e9),
        name="slice_rows",
    )(rows, tok, o)


CW = 1024
AHEAD = 2
FAR, NEAR = 1, 0


def pack_kernel(jobs, ne, cg, nep, n, *refs):
    nj = len(jobs)
    nsib = 1 + max(job[4] for job in jobs)
    o = refs[1]
    sibs, tabs = refs[2:2 + nsib], refs[2 + nsib:4 + nsib]
    outs = refs[4 + nsib:4 + nsib + nj]
    _, in_s, out_s, sel_ref, tab_ref, isem, osem, tsem = refs[4 + nsib + nj:]
    j = lax.axis_index('ep')
    firsts = (j * cg, lax.rem(j + nep // 2, nep) * cg)

    def fetch(i, c, slot):
        m, which, _, _, s, ms = jobs[i]
        cs = pl.ds(pl.multiple_of(c * CW, CW), CW)
        rs = pl.ds(pl.multiple_of(firsts[which], 16), cg)
        src = [o.at[m, e, rs, cs] for e in range(ne)]
        src += [sibs[s].at[ms, which, e, :, cs] for e in range(ne)]
        return [pltpu.make_async_copy(v, in_s.at[slot, pl.ds(e * cg, cg)], isem.at[slot, e]) for e, v in enumerate(src)]

    def put(i, c, slot):
        ls = pl.ds(pl.multiple_of(c * CW, CW), CW)
        return pltpu.make_async_copy(out_s.at[slot, pl.ds(0, jobs[i][3])], outs[i].at[:, ls], osem.at[slot])

    def at(i, c, f):
        for k, lo in ((i - 1, -n), (i, 0), (i + 1, n)):
            if 0 <= k < nj:
                @pl.when(jnp.logical_and(c >= lo, c < lo + n))
                def _():
                    f(k, c - lo, i * n + c)

    tables = [pltpu.make_async_copy(t, tab_ref.at[k], tsem.at[k]) for k, t in enumerate(tabs)]
    for t in tables:
        t.start()
    for t in range(min(AHEAD, nj * n)):
        for x in fetch(t // n, t % n, t):
            x.start()
    for t in tables:
        t.wait()
    for i, (m, which, row0, nr, _, _) in enumerate(jobs):
        col = jnp.transpose(tab_ref[which])[row0:row0 + nr, m:m + 1]
        r = lax.broadcasted_iota(jnp.int32, (nr, 2 * ne * cg), 1).astype(F32)
        sel_ref[:nr] = jnp.where(col == r, 1.0, 0.0).astype(BF16)

        def step(c, _):
            t = i * n + c
            for x in fetch(i, c, lax.rem(t, AHEAD + 1)):
                x.wait()

            def ahead(k, ck, tk):
                for x in fetch(k, ck, lax.rem(tk, AHEAD + 1)):
                    x.start()

            at(i, c + AHEAD, ahead)
            at(i, c - 2, lambda k, ck, tk: put(k, ck, lax.rem(tk, 2)).wait())
            rows = in_s[lax.rem(t, AHEAD + 1)]
            out_s[lax.rem(t, 2), :nr] = jnp.dot(sel_ref[:nr], rows, preferred_element_type=F32).astype(BF16)
            put(i, c, lax.rem(t, 2)).start()
            return 0

        lax.fori_loop(0, n, step, 0)
    for t in range(max(0, nj * n - 2), nj * n):
        put(t // n, t % n, t % 2).wait()


def pack(tok, o, sib, tabs, jobs, cg):
    _, ne, cap, d = o.shape
    arrays, full = [], []
    for job in jobs:
        a, ms = sib[job[0]]
        k = next((k for k, b in enumerate(arrays) if b is a), len(arrays))
        if k == len(arrays):
            arrays.append(a)
        full.append((*job, k, ms))
    n = d // CW
    most = max(job[3] for job in jobs)
    return pl.pallas_call(
        functools.partial(pack_kernel, full, ne, cg, cap // cg, n),
        in_specs=[ANY] * (4 + len(arrays)),
        out_specs=[ANY] * (len(jobs) + 1),
        out_shape=[jax.ShapeDtypeStruct((job[3], d), BF16) for job in jobs] + [TOK],
        input_output_aliases={0: len(jobs)},
        scratch_shapes=[pltpu.VMEM((AHEAD + 1, 2 * ne * cg, CW), BF16), pltpu.VMEM((2, most, CW), BF16),
                        pltpu.VMEM((most, 2 * ne * cg), BF16), pltpu.VMEM((2,) + tabs[0].shape, F32),
                        pltpu.SemaphoreType.DMA((AHEAD + 1, 2 * ne)), pltpu.SemaphoreType.DMA((2,)),
                        pltpu.SemaphoreType.DMA((2,))],
        compiler_params=pltpu.CompilerParams(vmem_limit_bytes=VMEM_LIMIT),
        cost_estimate=cost(2 * most * 2 * ne * cg * d * len(jobs)),
        name="pack",
    )(tok, o, *arrays, *tabs)


TB = 128
KW = 256


def combine_kernel(m, starts, tok, h, near, far, rest, tab, out, tok_out, h_s, near_s, far_s, out_s, sel_ref, gate_ref,
                   rank_ref, tab_ref, st_ref, isem, osem, tsem, rsem):
    nt, ncol = out_s.shape
    nb, full, fr = nt // TB, near_s.shape[0], far.shape[0]
    n = ncol // CW
    packed = (near_s, far_s)

    def fetch(c):
        ls = pl.ds(pl.multiple_of(c * CW, CW), CW)
        pairs = [(near.at[:, ls], near_s.at[:, ls]), (far.at[:, ls], far_s.at[pl.ds(0, fr), ls]),
                 (h.at[m, 0, :, ls], h_s.at[:, ls])]
        return [pltpu.make_async_copy(s, t, isem.at[c, e]) for e, (s, t) in enumerate(pairs)]

    def put(c):
        ls = pl.ds(pl.multiple_of(c * CW, CW), CW)
        return pltpu.make_async_copy(out_s.at[:, ls], out.at[:, ls], osem.at[c])

    def windows(b):
        ws, more = [], False
        for q in range(2):
            start, count = st_ref[((m * nb + b) * 2 + q) * 2], st_ref[((m * nb + b) * 2 + q) * 2 + 1]
            w = jnp.minimum(start - lax.rem(start, 16), full - KW)
            ws.append(pl.multiple_of(w, 16))
            more = jnp.logical_or(more, start + count > w + KW)
        return ws, more

    small = [pltpu.make_async_copy(tab.at[m], tab_ref, tsem.at[0]), pltpu.make_async_copy(starts, st_ref, tsem.at[1])]
    for x in small:
        x.start()
    for c in range(min(AHEAD, n)):
        for x in fetch(c):
            x.start()
    for x in small:
        x.wait()
    over = st_ref[st_ref.shape[0] - 1] > 0
    if fr < full:
        @pl.when(over)
        def _():
            x = pltpu.make_async_copy(rest, far_s.at[pl.ds(fr, full - fr)], rsem)
            x.start()
            x.wait()

        @pl.when(jnp.logical_not(over))
        def _():
            far_s[fr:, :] = jnp.zeros_like(far_s[fr:, :])

    cols = jnp.transpose(tab_ref[...])
    iw = lax.broadcasted_iota(jnp.int32, (TB, KW), 1).astype(F32)
    for k in range(2):
        gate_ref[k] = jnp.broadcast_to(cols[:, 4 + k:5 + k], (nt, 128))
        for q in range(2):
            rank_ref[k, q] = jnp.broadcast_to(cols[:, 2 * q + k:2 * q + k + 1], (nt, 128))
    for b in range(nb):
        ws, _ = windows(b)
        for k in range(2):
            for q in range(2):
                r = cols[b * TB:(b + 1) * TB, 2 * q + k:2 * q + k + 1] - ws[q].astype(F32)
                sel_ref[b, k * TB:(k + 1) * TB, q * KW:(q + 1) * KW] = jnp.where(r == iw, 1.0, 0.0).astype(BF16)

    def step(c, _):
        for x in fetch(c):
            x.wait()

        @pl.when(c + AHEAD < n)
        def _():
            for x in fetch(c + AHEAD):
                x.start()

        ls = pl.ds(pl.multiple_of(c * CW, CW), CW)

        def rows(ws):
            return jnp.concatenate([packed[q][pl.ds(ws[q], KW), ls] for q in range(2)], axis=0)

        for b in range(nb):
            ts = slice(b * TB, (b + 1) * TB)
            r = jnp.dot(sel_ref[b], rows(windows(b)[0]), preferred_element_type=F32)
            acc = h_s[ts, ls].astype(F32)
            for k in range(2):
                acc = acc + gate_ref[k, ts, :1] * r[k * TB:(k + 1) * TB]
            out_s[ts, ls] = acc.astype(BF16)

        def past(b, _):
            ws, more = windows(b)

            @pl.when(more)
            def _():
                ts = pl.ds(pl.multiple_of(b * TB, TB), TB)
                vs = [pl.multiple_of(jnp.minimum(w + KW, full - KW), 16) for w in ws]
                acc = h_s[ts, ls].astype(F32)
                for k in range(2):
                    sel = []
                    for q in range(2):
                        r = rank_ref[k, q, ts, :1]
                        r = jnp.where(r >= (ws[q] + KW).astype(F32), r - vs[q].astype(F32), -1.0)
                        sel.append(jnp.where(r == iw, 1.0, 0.0).astype(BF16))
                    r = jnp.dot(jnp.concatenate(sel, axis=1), rows(vs), preferred_element_type=F32)
                    r += jnp.dot(sel_ref[b, k * TB:(k + 1) * TB], rows(ws), preferred_element_type=F32)
                    acc = acc + gate_ref[k, ts, :1] * r
                out_s[ts, ls] = acc.astype(BF16)

            return 0

        lax.fori_loop(0, nb, past, 0)
        put(c).start()
        return 0

    lax.fori_loop(0, n, step, 0)
    for c in range(n):
        put(c).wait()


def combine(starts, tok, h, near, far, rest, tab, m):
    nt, d = h.shape[2:]
    full = near.shape[0]
    n = d // CW
    return pl.pallas_call(
        functools.partial(combine_kernel, m),
        in_specs=[ANY] * 7,
        out_specs=[ANY, ANY],
        out_shape=[jax.ShapeDtypeStruct((nt, d), BF16), TOK],
        input_output_aliases={1: 1},
        scratch_shapes=[pltpu.VMEM((nt, d), BF16), pltpu.VMEM((full, d), BF16), pltpu.VMEM((full, d), BF16),
                        pltpu.VMEM((nt, d), BF16), pltpu.VMEM((nt // TB, 2 * TB, 2 * KW), BF16),
                        pltpu.VMEM((2, nt, 128), F32), pltpu.VMEM((2, 2, nt, 128), F32),
                        pltpu.VMEM(tab.shape[1:], F32), pltpu.SMEM(starts.shape, jnp.int32),
                        pltpu.SemaphoreType.DMA((n, 3)), pltpu.SemaphoreType.DMA((n,)), pltpu.SemaphoreType.DMA((2,)),
                        pltpu.SemaphoreType.DMA],
        compiler_params=pltpu.CompilerParams(vmem_limit_bytes=VMEM_LIMIT),
        cost_estimate=cost(4 * nt * 2 * KW * d),
        name="combine",
    )(starts, tok, h, near, far, rest, tab)


def nothing_kernel(tok, *refs):
    pass


def nothing(tok, shapes):
    return pl.pallas_call(nothing_kernel, in_specs=[ANY], out_specs=[ANY] * (len(shapes) + 1),
                          out_shape=[jax.ShapeDtypeStruct(s, BF16) for s in shapes] + [TOK],
                          input_output_aliases={0: len(shapes)}, name="nothing")(tok)


G = 4
QB = 256
NR = 6


def scores(q, k, h, p_s, l_s):
    nt = q.shape[0]
    sc = (HD ** -0.5) * math.log2(math.e)
    off = 0
    for q0 in range(0, nt, QB):
        kn = q0 + QB
        s = lax.dot_general(q[q0:kn], k[:kn], (((1,), (1,)), ((), ())), preferred_element_type=F32)
        r = lax.broadcasted_iota(jnp.int32, (QB, QB), 0)
        c = lax.broadcasted_iota(jnp.int32, (QB, QB), 1)
        sd = jnp.where(r >= c, s[:, q0:], -1e30)
        s = sd if q0 == 0 else jnp.concatenate([s[:, :q0], sd], axis=1)
        mx = jnp.max(s, axis=1, keepdims=True)
        p = jnp.exp2(s * sc - mx * sc)
        p_s[h, :, off:off + kn] = p
        l_s[h, q0:kn, :] = jnp.broadcast_to(jnp.sum(p, axis=1, keepdims=True), (QB, HD))
        off += kn


def layer_kernel(first, npiece, *refs):
    us, refs = refs[:npiece], refs[npiece:]
    if not first:
        refs = refs[1:]
    (m_ref, _, w_ref, wq, wk, wv, wo, z_hbm, _, u_s, x_s, a_s, q_s, k_s, v_s, z_s, p_s, l_s, ring, rsem, usem,
     zsem) = refs
    nt, d = u_s.shape
    m = m_ref[0]
    gc = G * HD
    ng = d // gc
    uc = 4
    if npiece == 1:
        cr = nt // uc
        ucp = [pltpu.make_async_copy(us[0].at[pl.ds(c * cr, cr)], u_s.at[pl.ds(c * cr, cr)], usem.at[c])
               for c in range(uc)]
    else:
        cw = d // npiece
        ucp = [pltpu.make_async_copy(us[c], u_s.at[:, pl.ds(c * cw, cw)], usem.at[c]) for c in range(npiece)]
    for c in ucp:
        c.start()

    def wcopy(ref, col, slot):
        return pltpu.make_async_copy(ref.at[:, pl.ds(pl.multiple_of(col * gc, gc), gc)], ring.at[slot], rsem.at[slot])

    def qkv_start(i):
        b = lax.rem(i, 2) * 3
        for c, r in enumerate((wq, wk, wv)):
            wcopy(r, i, b + c).start()

    def wo_start(j):
        wcopy(wo, j, lax.rem(3 * ng + j, NR)).start()

    def wait(slot):
        wcopy(wq, 0, slot).wait()

    qkv_start(0)
    ch = 64

    def norm(r0, n):
        def f(t, _):
            rs = pl.ds(pl.multiple_of(r0 + t * ch, ch), ch)
            uf = u_s[rs, :].astype(F32)
            x_s[rs, :] = (uf * lax.rsqrt(jnp.mean(uf * uf, axis=-1, keepdims=True) + EPS) * w_ref[...]).astype(BF16)
            return 0

        lax.fori_loop(0, n // ch, f, 0)

    for c in range(len(ucp)):
        ucp[c].wait()
        if npiece == 1:
            norm(c * cr, cr)
    if npiece > 1:
        norm(0, nt)

    def attend(i):
        for h in range(G):
            off = 0
            for q0 in range(0, nt, QB):
                kn = q0 + QB
                p = p_s[h, :, off:off + kn]
                off += kn
                v = v_s[:kn, h * HD:(h + 1) * HD].astype(F32)
                o = jnp.dot(p, v, preferred_element_type=F32) / l_s[h, q0:kn, :]
                a_s[q0:kn, pl.ds(pl.multiple_of(i * gc, gc) + h * HD, HD)] = o.astype(BF16)

    def group(i, _):
        b = lax.rem(i, 2) * 3
        for c in range(3):
            wait(b + c)

        @pl.when(i + 1 < ng)
        def _():
            qkv_start(i + 1)

        @pl.when(i + 1 >= ng)
        def _():
            for j in range(3):
                wo_start(j)

        attend(jnp.maximum(i - 1, 0))
        q_s[...] = jnp.dot(x_s[...], ring[b], preferred_element_type=F32).astype(BF16)
        k_s[...] = jnp.dot(x_s[...], ring[b + 1], preferred_element_type=F32).astype(BF16)
        for h in range(G):
            scores(q_s[:, h * HD:(h + 1) * HD], k_s[:, h * HD:(h + 1) * HD], h, p_s, l_s)
        v_s[...] = jnp.dot(x_s[...], ring[b + 2], preferred_element_type=F32).astype(BF16)
        return 0

    lax.fori_loop(0, ng, group, 0)
    wo_start(3)
    attend(ng - 1)

    def zcopy(j):
        cs = pl.ds(pl.multiple_of(j * gc, gc), gc)
        return pltpu.make_async_copy(z_s.at[:, cs], z_hbm.at[m, 0, :, cs], zsem.at[j])

    def wo_step(jj, _):
        for e in range(2):
            wait(lax.rem(3 * ng + jj * 2 + e, NR))
        for e in range(2):
            @pl.when(jj * 2 + e + 4 < ng)
            def _():
                wo_start(jj * 2 + e + 4)
        for e in range(2):
            j = jj * 2 + e
            y = jnp.dot(a_s[...], ring[lax.rem(3 * ng + j, NR)], preferred_element_type=F32).astype(BF16).astype(F32)
            cs = pl.ds(pl.multiple_of(j * gc, gc), gc)
            z_s[:, cs] = (u_s[:, cs].astype(F32) + y).astype(BF16)
        for e in range(2):
            zcopy(jj * 2 + e).start()
        return 0

    lax.fori_loop(0, ng // 2, wo_step, 0)
    for j in range(ng):
        zcopy(j).wait()


def layer(us, z, m, tok, w, wq, wk, wv, wo, mb):
    nt, d = us[0].shape[0], wq.shape[0]
    first = z is None
    n = len(us)
    ng = d // (G * HD)
    smem = pl.BlockSpec(memory_space=pltpu.SMEM)
    vmem = pl.BlockSpec(memory_space=pltpu.VMEM)
    ins = list(us) + ([] if first else [z]) + [jnp.full((1,), m, jnp.int32), tok, w, wq, wk, wv, wo]
    specs = [ANY] * n + ([] if first else [ANY]) + [smem, ANY, vmem] + [ANY] * 4
    alias = {} if first else {n: 0}
    alias[len(specs) - 6] = 1
    pw = sum(range(QB, nt + 1, QB))
    return pl.pallas_call(
        functools.partial(layer_kernel, first, n),
        in_specs=specs,
        out_specs=[ANY, ANY],
        out_shape=[jax.ShapeDtypeStruct((mb, 1, nt, d), BF16), TOK],
        input_output_aliases=alias,
        scratch_shapes=[pltpu.VMEM((nt, d), BF16)] * 3 + [pltpu.VMEM((nt, G * HD), BF16)] * 3 + [
            pltpu.VMEM((nt, d), BF16), pltpu.VMEM((G, QB, pw), F32), pltpu.VMEM((G, nt, HD), F32),
            pltpu.VMEM((NR, d, G * HD), BF16), pltpu.SemaphoreType.DMA((NR,)),
            pltpu.SemaphoreType.DMA((max(4, n),)), pltpu.SemaphoreType.DMA((ng,))],
        compiler_params=pltpu.CompilerParams(vmem_limit_bytes=VMEM_LIMIT),
        cost_estimate=cost(8 * nt * d * d + 4 * nt * nt * d),
        name="layer",
    )(*ins)


def tables(idx, slot, gate, x, c, j, ne, cg):
    mb, nt, top = idx.shape
    valid = slot >= 0
    core = (idx // ne) % 2
    row = jnp.where(core == c, 0, ne * cg) + (idx % ne) * cg + slot - j * cg
    row = row.reshape(mb, 1, nt * top)
    other = idx // (2 * ne) != x
    place = jnp.arange(2 * ne * cg, dtype=jnp.int32)[None, :, None]
    ranks, starts, rows, counts = [], [], [], []
    for mine in (valid & ~other, valid & other):
        flat = mine.reshape(mb, nt * top)
        rank = jnp.cumsum(flat.astype(jnp.int32), axis=1) - 1
        at = jnp.where(flat, rank, -1)
        ranks.append(at.reshape(mb, nt, top).astype(F32))
        count = flat.reshape(mb, nt // TB, TB * top).sum(-1, dtype=jnp.int32)
        starts.append(jnp.stack([jnp.cumsum(count, axis=1) - count, count], axis=-1))
        rows.append((jnp.sum(jnp.where(at[:, None, :] == place, row + 1, 0), axis=-1) - 1).astype(F32))
        counts.append(count.sum(-1))
    cols = jnp.stack([v[..., k] for v in (*ranks, gate) for k in range(top)], axis=1)
    return cols, jnp.stack(starts, axis=2), rows, jnp.maximum(*counts)


CAP = 576


def order(mb):
    r = [('r', k, k) for k in range(3)]
    c = [('c', m, m) for m in range(mb)]
    half = (mb + 2) // 2
    out = [('p', 0, 1), ('s', 1, 2)] + r[:1] + [('b', 0, 2), ('e', 0, 2), ('s', 2, mb)] + r[1:2] + c[:1] + r[2:]
    out += [('b', 2, half), ('b', half, mb), ('e', 2, mb)] + c[1:2]
    for m in range(mb):
        out += [('l', m, m)]
        if m + 2 < mb:
            out += c[m + 2:m + 3]
    return out


def solution(mesh):
    npp, nep = mesh.shape['pp'], mesh.shape['ep']
    over = [(i, (i + 1) % npp) for i in range(npp)]
    peer = [(i, (i + nep // 2) % nep) for i in range(nep)]
    sibling = [(i, i ^ 1) for i in range(nep)]
    tok_spec = P(('data', 'pp'), None, 'ep', None, None)
    wsp = P('pp', None, None, None)

    def body(O, idx, slot, g, H, w, Wq, Wk, Wv, Wo):
        o, h = O[0], H[0]
        mb, ne, cap, d = o.shape
        cg = cap // nep
        nt = h.shape[2]
        j = lax.axis_index('ep')
        x, c = j // 2, j % 2
        three = lambda a: a[0].reshape(mb, nt, a.shape[-1])
        cols, starts, rows, need = tables(three(idx), three(slot), three(g), x, c, j, ne, cg)
        send = jnp.stack([2 * x + 1 - c, (2 * x + 1 - c + 2) % nep]).astype(jnp.int32)
        fresh = jnp.zeros((8, 128), F32)
        wqkv = [a[0] for a in (Wq, Wk, Wv)]
        wo = Wo[0].reshape(d, d)

        full = 2 * ne * cg
        s0, tok = slice_rows(send, fresh, o, 0, 1, cg)
        d0 = lax.ppermute(s0, 'ep', sibling)
        tabs = [rows[NEAR], lax.ppermute(rows[FAR], 'ep', peer)]

        def run(tok, sib):
            over_cap = (need > CAP).astype(jnp.int32).max().reshape(1)
            for axis, pairs in (('ep', peer), ('pp', over), ('ep', sibling)):
                over_cap = jnp.maximum(over_cap, lax.ppermute(over_cap, axis, pairs))
            st = jnp.concatenate([starts.reshape(-1), jnp.broadcast_to(over_cap, (128,))])
            near, far, packed, rest, ys = {}, {}, {}, {}, {}
            z = None
            for kind, m, e in order(mb):
                if kind == 's':
                    s, tok = slice_rows(send, tok, o, m, e - m, cg)
                    s = lax.ppermute(s, 'ep', sibling)
                    for i in range(m, e):
                        sib[i] = (s, i - m)
                elif kind == 'r':
                    v, tok = lax.optimization_barrier((wqkv[m], tok))
                    wqkv[m], tok = lax.optimization_barrier((jnp.reshape(v, (d, d)), tok))
                elif kind in 'pb':
                    jobs = [(i, w_, 0, CAP if w_ == FAR else full) for i in range(m, e) for w_ in (FAR, NEAR)]
                    jobs = [b for b in jobs if (b[1] == FAR) == (kind == 'p') or b[0] > 0]
                    *out, tok = pack(tok, o, sib, tabs, jobs, cg)
                    for b, r in zip(jobs, out):
                        if b[1] == NEAR:
                            near[b[0]] = r
                        elif b[0] == 0:
                            far[0] = lax.ppermute(r, 'ep', peer)
                        else:
                            packed[b[0]] = r
                elif kind == 'e':
                    def past(tok):
                        *out, tok = pack(tok, o, sib, tabs, [(i, FAR, CAP, full - CAP) for i in range(m, e)], cg)
                        return [lax.ppermute(v, 'ep', peer) for v in out] + [tok]

                    def none(tok):
                        return list(nothing(tok, [(full - CAP, d)] * (e - m)))

                    *out, tok = lax.cond(over_cap[0] > 0, past, none, tok)
                    rest.update(zip(range(m, e), out))
                    for i in sorted(packed):
                        v, tok = lax.optimization_barrier((packed.pop(i), tok))
                        far[i] = lax.ppermute(v, 'ep', peer)
                elif kind == 'c':
                    y, tok = combine(st, tok, h, near[m], far[m], rest[m], cols, m)
                    ys[m] = [lax.ppermute(y, 'pp', over)]
                else:
                    z, tok = layer(ys[m], z, m, tok, w, *wqkv, wo, mb)
            return z

        return run(tok, {0: (d0, 0)})[None]

    return jax.shard_map(body, mesh=mesh,
                         in_specs=(tok_spec, tok_spec, tok_spec, tok_spec, tok_spec, P('pp', None), wsp, wsp, wsp, wsp),
                         out_specs=tok_spec, check_vma=False)
```

profile of v0, /device:TPU:0, one launch (start us, length us, event | category | flops | bytes accessed | tf_op | source)
XLA Modules:
  0.0 1531.2 jit_solution(9814088222983265419)
XLA Ops:
  0.0 0.6 pad_add_fusion.1.rows_ref
  0.6 5.1 slice_rows.3
  5.7 0.8 collective-permute-start.11
  6.8 0.2 copy.111
  7.1 0.4 fusion.19
  7.5 0.4 copy.118
  7.9 0.3 ge.43
  8.8 2.3 reduce-window.14
  11.1 0.3 slice_reduce_fusion.1
  11.6 2.3 reduce-window.16
  13.8 0.3 slice_reduce_fusion
  14.7 5.4 select_reduce_fusion
  20.2 2.5 collective-permute-start.12
  22.7 1.8 collective-permute-done.12.refs_4_.refs_5_
  24.5 6.9 pack.8
  31.4 4.9 slice_rows.4
  36.4 0.7 fusion.23
  37.1 2.0 collective-permute-start.8
  39.1 1.7 collective-permute-done.8
  42.1 3.3 collective-permute-start.9
  46.4 0.8 collective-permute-start.10
  47.2 0.3 collective-permute-done.10
  48.2 22.7 %copy.144 = bf16[512,8,32,128]{3,1,2,0:T(8,128)(2,1)} copy(bf16[512,8,32,128]{3,2,1,0:T(8,128)(2,1)} %bitcast.110) | data formatting | bytes 67108864
  70.9 17.7 %pack.9 = (bf16[640,4096]{1,0:T(8,128)(2,1)}, bf16[576,4096]{1,0:T(8,128)(2,1)}, bf16[640,4096]{1,0:T(8,128)(2,1)}, f32[8,128]{1,0:T(8,128)S(1)}) custom-call(f32[8,128]{1,0:T(8,128)S(1)} %get-tuple-element.149.refs_0_, bf16[8,2,640,4096]{3,2,1,0:T(8,128)(2,1)} %bitcast.15.o_ref.refs_1_, ...), custom_call_target="tpu_custom_call", output_to_operand_aliasing={{3}: (0, {})} | custom-call | flops 10066329600 | bytes 39321600 | tf_op jit(solution)/shard_map/pack/pallas_call | solution.py:127
  88.6 24.8 %slice_rows.5 = (bf16[6,2,2,160,4096]{4,3,2,1,0:T(8,128)(2,1)}, f32[8,128]{1,0:T(8,128)S(1)}) custom-call(s32[2]{0:T(128)} %pad_add_fusion.1.rows_ref, f32[8,128]{1,0:T(8,128)S(1)} %get-tuple-element.154.tok, bf16[8,2,640,4096]{3,2,1,0:T(8,128)(2,1)} %bitcast.15.o_ref.refs_1_), custom_call_target="tpu_custom_call", output_to_operand_aliasing={{1}: (1, {})} | custom-call | flops 12000000000 | bytes 46875000 | tf_op jit(solution)/shard_map/slice_rows/pallas_call | solution.py:32
  113.6 2.0 collective-permute-start.14
  117.7 0.8 stack.39.tab
  118.5 0.5 concatenate.3.starts
  119.0 22.6 %copy.143 = bf16[512,8,32,128]{3,1,2,0:T(8,128)(2,1)} copy(bf16[512,8,32,128]{3,2,1,0:T(8,128)(2,1)} %bitcast.111) | data formatting | bytes 67108864
  141.6 76.6 %collective-permute-done.14.far = bf16[576,4096]{1,0:T(8,128)(2,1)} collective-permute-done((bf16[576,4096]{1,0:T(8,128)(2,1)}, bf16[576,4096]{1,0:T(8,128)(2,1)}, u32[]{:S(2)}, u32[]{:S(2)}) %collective-permute-start.14) | collective-permute-done | bytes 4718624 | tf_op jit(solution)/shard_map/ppermute | solution.py:546
  218.2 10.5 combine.8
  228.7 22.7 %copy.142 = bf16[512,8,32,128]{3,1,2,0:T(8,128)(2,1)} copy(bf16[512,8,32,128]{3,2,1,0:T(8,128)(2,1)} %bitcast.112) | data formatting | bytes 67108864
  251.4 32.4 %pack.10 = (bf16[576,4096]{1,0:T(8,128)(2,1)}, bf16[640,4096]{1,0:T(8,128)(2,1)}, bf16[576,4096]{1,0:T(8,128)(2,1)}, bf16[640,4096]{1,0:T(8,128)(2,1)}, bf16[576...) custom-call(f32[8,128]{1,0:T(8,128)S(1)} %get-tuple-element.165.refs_0_, ...), custom_call_target="tpu_custom_call", output_to_operand_aliasing={{6}: (0, {})} | custom-call | flops 20132659200 | bytes 78643200 | tf_op jit(solution)/shard_map/pack/pallas_call | solution.py:127
  283.8 32.8 %pack.11 = (bf16[576,4096]{1,0:T(8,128)(2,1)}, bf16[640,4096]{1,0:T(8,128)(2,1)}, bf16[576,4096]{1,0:T(8,128)(2,1)}, bf16[640,4096]{1,0:T(8,128)(2,1)}, bf16[576...) custom-call(f32[8,128]{1,0:T(8,128)S(1)} %get-tuple-element.167.refs_0_, ...), custom_call_target="tpu_custom_call", output_to_operand_aliasing={{6}: (0, {})} | custom-call | flops 20132659200 | bytes 78643200 | tf_op jit(solution)/shard_map/pack/pallas_call | solution.py:127
  316.6 1.9 collective-permute-start.16
  318.5 1.5 collective-permute-start.18
  320.0 100.4 %collective-permute-done.16.far = bf16[576,4096]{1,0:T(8,128)(2,1)} collective-permute-done((bf16[576,4096]{1,0:T(8,128)(2,1)}, bf16[576,4096]{1,0:T(8,128)(2,1)}, u32[]{:S(2)}, u32[]{:S(2)}) %collective-permute-start.16) | collective-permute-done | bytes 4718624 | tf_op jit(solution)/shard_map/ppermute | solution.py:561
  420.3 10.7 combine.9
  431.0 1.5 collective-permute-start.17
  432.6 1.5 collective-permute-start.28
  434.1 0.5 collective-permute-start.27
  434.6 1.5 collective-permute-start.24
  436.1 0.5 collective-permute-start.19
  436.6 88.4 %layer.8 = (bf16[8,1,512,4096]{3,2,1,0:T(8,128)(2,1)}, f32[8,128]{1,0:T(8,128)S(1)}) custom-call(bf16[512,4096]{1,0:T(8,128)(2,1)} %collective-permute-done.18.refs_0_, s32[1]{0:T(128)} %constant.106.clone.1.refs_1_, f32[8,128]{1,0:T(8,128)S(1)} %get-tuple-element.187.refs_2_, f32[1,4096]{1,0:T(1,128)} %refs_4_.13, ...), custom_call_target="tpu_custom_call", output_to_operand_aliasing={{1}: (2, {})} | custom-call | flops 73014444032 | bytes 285212672 | tf_op jit(solution)/shard_map/layer/pallas_call | solution.py:441
  525.0 313.3 %collective-permute-done.19.far = bf16[576,4096]{1,0:T(8,128)(2,1)} collective-permute-done((bf16[576,4096]{1,0:T(8,128)(2,1)}, bf16[576,4096]{1,0:T(8,128)(2,1)}, u32[]{:S(2)}, u32[]{:S(2)}) %collective-permute-start.19) | collective-permute-done | bytes 4718624 | tf_op jit(solution)/shard_map/ppermute | solution.py:561
  838.3 1.4 collective-permute-start.20
  839.7 10.9 combine.10
  850.6 0.5 collective-permute-start.22
  851.1 88.4 %layer.9 = (bf16[8,1,512,4096]{3,2,1,0:T(8,128)(2,1)}, f32[8,128]{1,0:T(8,128)S(1)}) custom-call(bf16[512,4096]{1,0:T(8,128)(2,1)} %collective-permute-done.17.refs_0_, bf16[8,1,512,4096]{3,2,1,0:T(8,128)(2,1)} %get-tuple-element.191.refs_1_, s32[1]{0:T(128)} %constant.107.clone.1.refs_2_, ...), custom_call_target="tpu_custom_call", output_to_operand_aliasing={{0}: (1, {}), {1}: (3, {})} | custom-call | flops 73014444032 | bytes 285212672 | tf_op jit(solution)/shard_map/layer/pallas_call | solution.py:441
  939.5 0.7 collective-permute-done.20.far
  940.2 1.4 collective-permute-start.23
  941.7 11.1 combine.11
  952.8 88.4 %layer.10 = (bf16[8,1,512,4096]{3,2,1,0:T(8,128)(2,1)}, f32[8,128]{1,0:T(8,128)S(1)}) custom-call(bf16[512,4096]{1,0:T(8,128)(2,1)} %collective-permute-done.22.refs_0_, bf16[8,1,512,4096]{3,2,1,0:T(8,128)(2,1)} %get-tuple-element.203.refs_1_, s32[1]{0:T(128)} %constant.108.clone.1.refs_2_, ...), custom_call_target="tpu_custom_call", output_to_operand_aliasing={{0}: (1, {}), {1}: (3, {})} | custom-call | flops 73014444032 | bytes 285212672 | tf_op jit(solution)/shard_map/layer/pallas_call | solution.py:441
  1041.2 10.8 combine.12
  1052.1 2.0 collective-permute-start.26
  1054.1 88.4 %layer.11 = (bf16[8,1,512,4096]{3,2,1,0:T(8,128)(2,1)}, f32[8,128]{1,0:T(8,128)S(1)}) custom-call(bf16[512,4096]{1,0:T(8,128)(2,1)} %collective-permute-done.21.refs_0_, bf16[8,1,512,4096]{3,2,1,0:T(8,128)(2,1)} %get-tuple-element.205.refs_1_, s32[1]{0:T(128)} %constant.109.clone.1.refs_2_, ...), custom_call_target="tpu_custom_call", output_to_operand_aliasing={{0}: (1, {}), {1}: (3, {})} | custom-call | flops 73014444032 | bytes 285212672 | tf_op jit(solution)/shard_map/layer/pallas_call | solution.py:441
  1142.5 10.9 combine.13
  1153.5 88.4 %layer.12 = (bf16[8,1,512,4096]{3,2,1,0:T(8,128)(2,1)}, f32[8,128]{1,0:T(8,128)S(1)}) custom-call(bf16[512,4096]{1,0:T(8,128)(2,1)} %collective-permute-done.26.refs_0_, bf16[8,1,512,4096]{3,2,1,0:T(8,128)(2,1)} %get-tuple-element.217.refs_1_, s32[1]{0:T(128)} %constant.110.clone.1.refs_2_, ...), custom_call_target="tpu_custom_call", output_to_operand_aliasing={{0}: (1, {}), {1}: (3, {})} | custom-call | flops 73014444032 | bytes 285212672 | tf_op jit(solution)/shard_map/layer/pallas_call | solution.py:441
  1241.9 10.8 combine.14
  1252.7 2.0 collective-permute-start.30
  1254.7 88.4 %layer.13 = (bf16[8,1,512,4096]{3,2,1,0:T(8,128)(2,1)}, f32[8,128]{1,0:T(8,128)S(1)}) custom-call(bf16[512,4096]{1,0:T(8,128)(2,1)} %collective-permute-done.25.refs_0_, bf16[8,1,512,4096]{3,2,1,0:T(8,128)(2,1)} %get-tuple-element.219.refs_1_, s32[1]{0:T(128)} %constant.111.clone.1.refs_2_, ...), custom_call_target="tpu_custom_call", output_to_operand_aliasing={{0}: (1, {}), {1}: (3, {})} | custom-call | flops 73014444032 | bytes 285212672 | tf_op jit(solution)/shard_map/layer/pallas_call | solution.py:441
  1343.1 10.8 combine.15
  1354.0 88.4 %layer.14 = (bf16[8,1,512,4096]{3,2,1,0:T(8,128)(2,1)}, f32[8,128]{1,0:T(8,128)S(1)}) custom-call(bf16[512,4096]{1,0:T(8,128)(2,1)} %collective-permute-done.30.refs_0_, bf16[8,1,512,4096]{3,2,1,0:T(8,128)(2,1)} %get-tuple-element.231.refs_1_, s32[1]{0:T(128)} %constant.112.clone.1.refs_2_, ...), custom_call_target="tpu_custom_call", output_to_operand_aliasing={{0}: (1, {}), {1}: (3, {})} | custom-call | flops 73014444032 | bytes 285212672 | tf_op jit(solution)/shard_map/layer/pallas_call | solution.py:441
  1442.3 88.4 %layer.15 = (bf16[8,1,512,4096]{3,2,1,0:T(8,128)(2,1)}, f32[8,128]{1,0:T(8,128)S(1)}) custom-call(bf16[512,4096]{1,0:T(8,128)(2,1)} %collective-permute-done.29.refs_0_, bf16[8,1,512,4096]{3,2,1,0:T(8,128)(2,1)} %get-tuple-element.233.refs_1_, s32[1]{0:T(128)} %constant.113.clone.1.refs_2_, ...), custom_call_target="tpu_custom_call", output_to_operand_aliasing={{0}: (1, {}), {1}: (3, {})} | custom-call | flops 73014444032 | bytes 285212672 | tf_op jit(solution)/shard_map/layer/pallas_call | solution.py:441
  (69 shorter events, 4.2 us)
Async XLA Ops:
  0.6 5.9 copy-start
  0.6 6.2 copy-start.1
  5.7 18.7 %collective-permute-start.11 = (bf16[1,2,2,160,4096]{4,3,2,1,0:T(8,128)(2,1)}, bf16[1,2,2,160,4096]{4,3,2,1,0:T(8,128)(2,1)}, u32[]{:S(2)}, u32[]{:S(2)}) collective-permute-start(bf16[1,2,2,160,4096]{4,3,2,1,0:T(8,128)(2,1)} %get-tuple-element.144), channel_id=1, source_target_pairs={{0,1},{1,0},{2,3},{3,2},{4,5},{5,4},{6,7},{7,6}} | collective-permute-start | bytes 15728648 | tf_op jit(solution)/shard_map/ppermute | solution.py:519
  20.2 4.3 collective-permute-start.12
  36.4 34.5 %collective-permute-start.13 = (bf16[1,2,2,160,4096]{4,3,2,1,0:T(8,128)(2,1)}, bf16[1,2,2,160,4096]{4,3,2,1,0:T(8,128)(2,1)}, u32[]{:S(2)}, u32[]{:S(2)}) collective-permute-start(bf16[1,2,2,160,4096]{4,3,2,1,0:T(8,128)(2,1)} %get-tuple-element.150), channel_id=1, source_target_pairs={{0,1},{1,0},{2,3},{3,2},{4,5},{5,4},{6,7},{7,6}} | collective-permute-start | bytes 15728648 | tf_op jit(solution)/shard_map/ppermute | solution.py:532
  37.1 3.7 collective-permute-start.8
  42.1 3.5 collective-permute-start.9
  46.4 1.2 collective-permute-start.10
  88.6 29.0 %copy-start.2 = (f32[1,8,1,512,2]{3,4,2,1,0:T(2,128)S(1)}, f32[1,8,1,512,2]{3,4,2,1,0:T(2,128)}, u32[]{:S(2)}) copy-start(f32[1,8,1,512,2]{3,4,2,1,0:T(2,128)} %param.17) | copy-start | bytes 98308
  113.4 137.9 %collective-permute-start.15 = (bf16[6,2,2,160,4096]{4,3,2,1,0:T(8,128)(2,1)}, bf16[6,2,2,160,4096]{4,3,2,1,0:T(8,128)(2,1)}, u32[]{:S(2)}, u32[]{:S(2)}) collective-permute-start(bf16[6,2,2,160,4096]{4,3,2,1,0:T(8,128)(2,1)} %get-tuple-element.166), channel_id=1, source_target_pairs={{0,1},{1,0},{2,3},{3,2},{4,5},{5,4},{6,7},{7,6}} | collective-permute-start | bytes 94371848 | tf_op jit(solution)/shard_map/ppermute | solution.py:532
  113.6 104.6 %collective-permute-start.14 = (bf16[576,4096]{1,0:T(8,128)(2,1)}, bf16[576,4096]{1,0:T(8,128)(2,1)}, u32[]{:S(2)}, u32[]{:S(2)}) collective-permute-start(bf16[576,4096]{1,0:T(8,128)(2,1)} %get-tuple-element.160), channel_id=1, source_target_pairs={{0,2},{1,3},{2,0},{3,1},{4,6},{5,7},{6,4},{7,5}} | collective-permute-start | bytes 14155784 | tf_op jit(solution)/shard_map/ppermute | solution.py:546
  316.6 103.8 %collective-permute-start.16 = (bf16[576,4096]{1,0:T(8,128)(2,1)}, bf16[576,4096]{1,0:T(8,128)(2,1)}, u32[]{:S(2)}, u32[]{:S(2)}) collective-permute-start(bf16[576,4096]{1,0:T(8,128)(2,1)} %get-tuple-element.183), channel_id=1, source_target_pairs={{0,2},{1,3},{2,0},{3,1},{4,6},{5,7},{6,4},{7,5}} | collective-permute-start | bytes 14155784 | tf_op jit(solution)/shard_map/ppermute | solution.py:561
  318.5 117.6 %collective-permute-start.18 = (bf16[512,4096]{1,0:T(8,128)(2,1)}, bf16[512,4096]{1,0:T(8,128)(2,1)}, u32[]{:S(2)}, u32[]{:S(2)}) collective-permute-start(bf16[512,4096]{1,0:T(8,128)(2,1)} %get-tuple-element.186), channel_id=1, source_target_pairs={{0,4},{4,0},{1,5},{5,1},{2,6},{6,2},{3,7},{7,3}} | collective-permute-start | bytes 12582920 | tf_op jit(solution)/shard_map/ppermute | solution.py:564
  431.0 419.6 %collective-permute-start.17 = (bf16[512,4096]{1,0:T(8,128)(2,1)}, bf16[512,4096]{1,0:T(8,128)(2,1)}, u32[]{:S(2)}, u32[]{:S(2)}) collective-permute-start(bf16[512,4096]{1,0:T(8,128)(2,1)} %get-tuple-element.185), channel_id=1, source_target_pairs={{0,4},{4,0},{1,5},{5,1},{2,6},{6,2},{3,7},{7,3}} | collective-permute-start | bytes 12582920 | tf_op jit(solution)/shard_map/ppermute | solution.py:564
  432.6 910.5 %collective-permute-start.28 = (bf16[576,4096]{1,0:T(8,128)(2,1)}, bf16[576,4096]{1,0:T(8,128)(2,1)}, u32[]{:S(2)}, u32[]{:S(2)}) collective-permute-start(bf16[576,4096]{1,0:T(8,128)(2,1)} %get-tuple-element.227), channel_id=1, source_target_pairs={{0,2},{1,3},{2,0},{3,1},{4,6},{5,7},{6,4},{7,5}} | collective-permute-start | bytes 14155784 | tf_op jit(solution)/shard_map/ppermute | solution.py:561
  434.1 807.8 %collective-permute-start.27 = (bf16[576,4096]{1,0:T(8,128)(2,1)}, bf16[576,4096]{1,0:T(8,128)(2,1)}, u32[]{:S(2)}, u32[]{:S(2)}) collective-permute-start(bf16[576,4096]{1,0:T(8,128)(2,1)} %get-tuple-element.222), channel_id=1, source_target_pairs={{0,2},{1,3},{2,0},{3,1},{4,6},{5,7},{6,4},{7,5}} | collective-permute-start | bytes 14155784 | tf_op jit(solution)/shard_map/ppermute | solution.py:561
  434.6 707.9 %collective-permute-start.24 = (bf16[576,4096]{1,0:T(8,128)(2,1)}, bf16[576,4096]{1,0:T(8,128)(2,1)}, u32[]{:S(2)}, u32[]{:S(2)}) collective-permute-start(bf16[576,4096]{1,0:T(8,128)(2,1)} %get-tuple-element.213), channel_id=1, source_target_pairs={{0,2},{1,3},{2,0},{3,1},{4,6},{5,7},{6,4},{7,5}} | collective-permute-start | bytes 14155784 | tf_op jit(solution)/shard_map/ppermute | solution.py:561
  436.1 402.2 %collective-permute-start.19 = (bf16[576,4096]{1,0:T(8,128)(2,1)}, bf16[576,4096]{1,0:T(8,128)(2,1)}, u32[]{:S(2)}, u32[]{:S(2)}) collective-permute-start(bf16[576,4096]{1,0:T(8,128)(2,1)} %get-tuple-element.194), channel_id=1, source_target_pairs={{0,2},{1,3},{2,0},{3,1},{4,6},{5,7},{6,4},{7,5}} | collective-permute-start | bytes 14155784 | tf_op jit(solution)/shard_map/ppermute | solution.py:561
  838.3 102.0 %collective-permute-start.20 = (bf16[576,4096]{1,0:T(8,128)(2,1)}, bf16[576,4096]{1,0:T(8,128)(2,1)}, u32[]{:S(2)}, u32[]{:S(2)}) collective-permute-start(bf16[576,4096]{1,0:T(8,128)(2,1)} %get-tuple-element.199), channel_id=1, source_target_pairs={{0,2},{1,3},{2,0},{3,1},{4,6},{5,7},{6,4},{7,5}} | collective-permute-start | bytes 14155784 | tf_op jit(solution)/shard_map/ppermute | solution.py:561
  850.6 102.2 %collective-permute-start.22 = (bf16[512,4096]{1,0:T(8,128)(2,1)}, bf16[512,4096]{1,0:T(8,128)(2,1)}, u32[]{:S(2)}, u32[]{:S(2)}) collective-permute-start(bf16[512,4096]{1,0:T(8,128)(2,1)} %get-tuple-element.202), channel_id=1, source_target_pairs={{0,4},{4,0},{1,5},{5,1},{2,6},{6,2},{3,7},{7,3}} | collective-permute-start | bytes 12582920 | tf_op jit(solution)/shard_map/ppermute | solution.py:564
  940.2 101.0 %collective-permute-start.23 = (bf16[576,4096]{1,0:T(8,128)(2,1)}, bf16[576,4096]{1,0:T(8,128)(2,1)}, u32[]{:S(2)}, u32[]{:S(2)}) collective-permute-start(bf16[576,4096]{1,0:T(8,128)(2,1)} %get-tuple-element.208), channel_id=1, source_target_pairs={{0,2},{1,3},{2,0},{3,1},{4,6},{5,7},{6,4},{7,5}} | collective-permute-start | bytes 14155784 | tf_op jit(solution)/shard_map/ppermute | solution.py:561
  952.8 101.3 %collective-permute-start.21 = (bf16[512,4096]{1,0:T(8,128)(2,1)}, bf16[512,4096]{1,0:T(8,128)(2,1)}, u32[]{:S(2)}, u32[]{:S(2)}) collective-permute-start(bf16[512,4096]{1,0:T(8,128)(2,1)} %get-tuple-element.201), channel_id=1, source_target_pairs={{0,4},{4,0},{1,5},{5,1},{2,6},{6,2},{3,7},{7,3}} | collective-permute-start | bytes 12582920 | tf_op jit(solution)/shard_map/ppermute | solution.py:564
  1052.1 101.4 %collective-permute-start.26 = (bf16[512,4096]{1,0:T(8,128)(2,1)}, bf16[512,4096]{1,0:T(8,128)(2,1)}, u32[]{:S(2)}, u32[]{:S(2)}) collective-permute-start(bf16[512,4096]{1,0:T(8,128)(2,1)} %get-tuple-element.216), channel_id=1, source_target_pairs={{0,4},{4,0},{1,5},{5,1},{2,6},{6,2},{3,7},{7,3}} | collective-permute-start | bytes 12582920 | tf_op jit(solution)/shard_map/ppermute | solution.py:564
  1153.4 101.3 %collective-permute-start.25 = (bf16[512,4096]{1,0:T(8,128)(2,1)}, bf16[512,4096]{1,0:T(8,128)(2,1)}, u32[]{:S(2)}, u32[]{:S(2)}) collective-permute-start(bf16[512,4096]{1,0:T(8,128)(2,1)} %get-tuple-element.215), channel_id=1, source_target_pairs={{0,4},{4,0},{1,5},{5,1},{2,6},{6,2},{3,7},{7,3}} | collective-permute-start | bytes 12582920 | tf_op jit(solution)/shard_map/ppermute | solution.py:564
  1252.7 101.2 %collective-permute-start.30 = (bf16[512,4096]{1,0:T(8,128)(2,1)}, bf16[512,4096]{1,0:T(8,128)(2,1)}, u32[]{:S(2)}, u32[]{:S(2)}) collective-permute-start(bf16[512,4096]{1,0:T(8,128)(2,1)} %get-tuple-element.230), channel_id=1, source_target_pairs={{0,4},{4,0},{1,5},{5,1},{2,6},{6,2},{3,7},{7,3}} | collective-permute-start | bytes 12582920 | tf_op jit(solution)/shard_map/ppermute | solution.py:564
  1353.9 88.4 %collective-permute-start.29 = (bf16[512,4096]{1,0:T(8,128)(2,1)}, bf16[512,4096]{1,0:T(8,128)(2,1)}, u32[]{:S(2)}, u32[]{:S(2)}) collective-permute-start(bf16[512,4096]{1,0:T(8,128)(2,1)} %get-tuple-element.229), channel_id=1, source_target_pairs={{0,4},{4,0},{1,5},{5,1},{2,6},{6,2},{3,7},{7,3}} | collective-permute-start | bytes 12582920 | tf_op jit(solution)/shard_map/ppermute | solution.py:564
where the time goes:
time: 1540 us; the launch traced here: 1530 us
  Pallas kernels  918 us (60%)
  waiting for transfers between devices  495 us (32%)
  local copies, waits for them, and re-layouts  73.2 us (5%)
  starting transfers between devices  28.2 us (2%)
    pallas_call x8, Pallas kernels, layer(): pl.pallas_call(functools.partial(layer_kernel, first, n), in_specs=specs,...  707 us
    ppermute x7, waiting for transfers between devices, run(): far[i] = lax.ppermute(v, 'ep', peer)  414 us
    pallas_call x4, Pallas kernels, pack(): pl.pallas_call(functools.partial(pack_kernel, full, ne, cg, cap // cg, n)...  89.8 us
    pallas_call x8, Pallas kernels, combine(): pl.pallas_call(functools.partial(combine_kernel, m), in_specs=[ANY] * 7,...  86.5 us
    ppermute x1, waiting for transfers between devices, run(): far[0] = lax.ppermute(r, 'ep', peer)  76.6 us
    unnamed x11, local copies, waits for them, and re-layouts  68.5 us
    pallas_call x3, Pallas kernels, slice_rows(): pl.pallas_call(slice_kernel, grid_spec=pltpu.PrefetchScalarGridSpec(num_s...  34.8 us
  transfers between devices with their start and end apart: 23, of which 8 were waited for; matrix products, arithmetic and copies ran while one was open for 6% of the time, Pallas kernels for 46%

commit v1 on v0

--- a/solution.py
+++ b/solution.py
@@ -14,7 +14,7 @@
 F32 = jnp.float32
 BF16 = jnp.bfloat16
 VMEM_LIMIT = 63 * 1024 * 1024
-ANY = pl.BlockSpec(memory_space=pl.ANY)
+ANY = pl.BlockSpec(memory_space=pltpu.HBM)
 TOK = jax.ShapeDtypeStruct((8, 128), F32)
 
 
@@ -45,6 +45,7 @@
     )(rows, tok, o)
 
 
+PW = 2048
 CW = 1024
 AHEAD = 2
 FAR, NEAR = 1, 0
@@ -62,14 +63,14 @@
 
     def fetch(i, c, slot):
         m, which, _, _, s, ms = jobs[i]
-        cs = pl.ds(pl.multiple_of(c * CW, CW), CW)
+        cs = pl.ds(pl.multiple_of(c * PW, PW), PW)
         rs = pl.ds(pl.multiple_of(firsts[which], 16), cg)
         src = [o.at[m, e, rs, cs] for e in range(ne)]
         src += [sibs[s].at[ms, which, e, :, cs] for e in range(ne)]
         return [pltpu.make_async_copy(v, in_s.at[slot, pl.ds(e * cg, cg)], isem.at[slot, e]) for e, v in enumerate(src)]
 
     def put(i, c, slot):
-        ls = pl.ds(pl.multiple_of(c * CW, CW), CW)
+        ls = pl.ds(pl.multiple_of(c * PW, PW), PW)
         return pltpu.make_async_copy(out_s.at[slot, pl.ds(0, jobs[i][3])], outs[i].at[:, ls], osem.at[slot])
 
     def at(i, c, f):
@@ -122,7 +123,7 @@
         if k == len(arrays):
             arrays.append(a)
         full.append((*job, k, ms))
-    n = d // CW
+    n = d // PW
     most = max(job[3] for job in jobs)
     return pl.pallas_call(
         functools.partial(pack_kernel, full, ne, cg, cap // cg, n),
@@ -130,7 +131,7 @@
         out_specs=[ANY] * (len(jobs) + 1),
         out_shape=[jax.ShapeDtypeStruct((job[3], d), BF16) for job in jobs] + [TOK],
         input_output_aliases={0: len(jobs)},
-        scratch_shapes=[pltpu.VMEM((AHEAD + 1, 2 * ne * cg, CW), BF16), pltpu.VMEM((2, most, CW), BF16),
+        scratch_shapes=[pltpu.VMEM((AHEAD + 1, 2 * ne * cg, PW), BF16), pltpu.VMEM((2, most, PW), BF16),
                         pltpu.VMEM((most, 2 * ne * cg), BF16), pltpu.VMEM((2,) + tabs[0].shape, F32),
                         pltpu.SemaphoreType.DMA((AHEAD + 1, 2 * ne)), pltpu.SemaphoreType.DMA((2,)),
                         pltpu.SemaphoreType.DMA((2,))],
@@ -142,18 +143,20 @@
 
 TB = 128
 KW = 256
-
-
-def combine_kernel(m, starts, tok, h, near, far, rest, tab, out, tok_out, h_s, near_s, far_s, out_s, sel_ref, gate_ref,
+NST = 128
+CAHEAD = 2
+
+
+def combine_kernel(m, full, starts, tok, h, near, far, near_rest, far_rest, tab, out, tok_out, h_s, near_s, far_s, out_s, sel_ref, gate_ref,
                    rank_ref, tab_ref, st_ref, isem, osem, tsem, rsem):
     nt, ncol = out_s.shape
-    nb, full, fr = nt // TB, near_s.shape[0], far.shape[0]
+    nb, cap = nt // TB, near.shape[0]
     n = ncol // CW
     packed = (near_s, far_s)
 
     def fetch(c):
         ls = pl.ds(pl.multiple_of(c * CW, CW), CW)
-        pairs = [(near.at[:, ls], near_s.at[:, ls]), (far.at[:, ls], far_s.at[pl.ds(0, fr), ls]),
+        pairs = [(near.at[:, ls], near_s.at[pl.ds(0, cap), ls]), (far.at[:, ls], far_s.at[pl.ds(0, cap), ls]),
                  (h.at[m, 0, :, ls], h_s.at[:, ls])]
         return [pltpu.make_async_copy(s, t, isem.at[c, e]) for e, (s, t) in enumerate(pairs)]
 
@@ -164,31 +167,35 @@
     def windows(b):
         ws, more = [], False
         for q in range(2):
-            start, count = st_ref[((m * nb + b) * 2 + q) * 2], st_ref[((m * nb + b) * 2 + q) * 2 + 1]
+            start, count = st_ref[(b * 2 + q) * 2], st_ref[(b * 2 + q) * 2 + 1]
             w = jnp.minimum(start - lax.rem(start, 16), full - KW)
             ws.append(pl.multiple_of(w, 16))
             more = jnp.logical_or(more, start + count > w + KW)
         return ws, more
 
-    small = [pltpu.make_async_copy(tab.at[m], tab_ref, tsem.at[0]), pltpu.make_async_copy(starts, st_ref, tsem.at[1])]
+    small = [pltpu.make_async_copy(tab.at[m], tab_ref, tsem.at[0]), pltpu.make_async_copy(starts.at[pl.ds(m * 128, NST)], st_ref, tsem.at[1])]
     for x in small:
         x.start()
-    for c in range(min(AHEAD, n)):
+    for c in range(min(CAHEAD, n)):
         for x in fetch(c):
             x.start()
     for x in small:
         x.wait()
-    over = st_ref[st_ref.shape[0] - 1] > 0
-    if fr < full:
+    over = st_ref[nb * 4] > 0
+    if cap < full:
         @pl.when(over)
         def _():
-            x = pltpu.make_async_copy(rest, far_s.at[pl.ds(fr, full - fr)], rsem)
-            x.start()
-            x.wait()
+            past = [pltpu.make_async_copy(r, p.at[pl.ds(cap, full - cap)], rsem.at[q])
+                    for q, (r, p) in enumerate(zip((near_rest, far_rest), packed))]
+            for x in past:
+                x.start()
+            for x in past:
+                x.wait()
 
         @pl.when(jnp.logical_not(over))
         def _():
-            far_s[fr:, :] = jnp.zeros_like(far_s[fr:, :])
+            for p in packed:
+                p[cap:, :] = jnp.zeros_like(p[cap:, :])
 
     cols = jnp.transpose(tab_ref[...])
     iw = lax.broadcasted_iota(jnp.int32, (TB, KW), 1).astype(F32)
@@ -207,9 +214,9 @@
         for x in fetch(c):
             x.wait()
 
-        @pl.when(c + AHEAD < n)
+        @pl.when(c + CAHEAD < n)
         def _():
-            for x in fetch(c + AHEAD):
+            for x in fetch(c + CAHEAD):
                 x.start()
 
         ls = pl.ds(pl.multiple_of(c * CW, CW), CW)
@@ -255,26 +262,25 @@
         put(c).wait()
 
 
-def combine(starts, tok, h, near, far, rest, tab, m):
+def combine(starts, tok, h, near, far, near_rest, far_rest, tab, m, full):
     nt, d = h.shape[2:]
-    full = near.shape[0]
     n = d // CW
     return pl.pallas_call(
-        functools.partial(combine_kernel, m),
-        in_specs=[ANY] * 7,
+        functools.partial(combine_kernel, m, full),
+        in_specs=[ANY] * 8,
         out_specs=[ANY, ANY],
         out_shape=[jax.ShapeDtypeStruct((nt, d), BF16), TOK],
         input_output_aliases={1: 1},
         scratch_shapes=[pltpu.VMEM((nt, d), BF16), pltpu.VMEM((full, d), BF16), pltpu.VMEM((full, d), BF16),
                         pltpu.VMEM((nt, d), BF16), pltpu.VMEM((nt // TB, 2 * TB, 2 * KW), BF16),
                         pltpu.VMEM((2, nt, 128), F32), pltpu.VMEM((2, 2, nt, 128), F32),
-                        pltpu.VMEM(tab.shape[1:], F32), pltpu.SMEM(starts.shape, jnp.int32),
+                        pltpu.VMEM(tab.shape[1:], F32), pltpu.SMEM((NST,), jnp.int32),
                         pltpu.SemaphoreType.DMA((n, 3)), pltpu.SemaphoreType.DMA((n,)), pltpu.SemaphoreType.DMA((2,)),
-                        pltpu.SemaphoreType.DMA],
+                        pltpu.SemaphoreType.DMA((2,))],
         compiler_params=pltpu.CompilerParams(vmem_limit_bytes=VMEM_LIMIT),
         cost_estimate=cost(4 * nt * 2 * KW * d),
         name="combine",
-    )(starts, tok, h, near, far, rest, tab)
+    )(starts, tok, h, near, far, near_rest, far_rest, tab)
 
 
 def nothing_kernel(tok, *refs):
@@ -310,14 +316,13 @@
         off += kn
 
 
-def layer_kernel(first, npiece, *refs):
+def layer_kernel(m, first, npiece, *refs):
     us, refs = refs[:npiece], refs[npiece:]
     if not first:
         refs = refs[1:]
-    (m_ref, _, w_ref, wq, wk, wv, wo, z_hbm, _, u_s, x_s, a_s, q_s, k_s, v_s, z_s, p_s, l_s, ring, rsem, usem,
-     zsem) = refs
+    (_, w, wq, wk, wv, wo, z_hbm, _, u_s, x_s, a_s, q_s, k_s, v_s, z_s, p_s, l_s, ring, w_ref, rsem, usem, zsem,
+     wsem) = refs
     nt, d = u_s.shape
-    m = m_ref[0]
     gc = G * HD
     ng = d // gc
     uc = 4
@@ -328,6 +333,8 @@
     else:
         cw = d // npiece
         ucp = [pltpu.make_async_copy(us[c], u_s.at[:, pl.ds(c * cw, cw)], usem.at[c]) for c in range(npiece)]
+    gain = pltpu.make_async_copy(w, w_ref, wsem)
+    gain.start()
     for c in ucp:
         c.start()
 
@@ -357,6 +364,7 @@
 
         lax.fori_loop(0, n // ch, f, 0)
 
+    gain.wait()
     for c in range(len(ucp)):
         ucp[c].wait()
         if npiece == 1:
@@ -431,23 +439,20 @@
     first = z is None
     n = len(us)
     ng = d // (G * HD)
-    smem = pl.BlockSpec(memory_space=pltpu.SMEM)
-    vmem = pl.BlockSpec(memory_space=pltpu.VMEM)
-    ins = list(us) + ([] if first else [z]) + [jnp.full((1,), m, jnp.int32), tok, w, wq, wk, wv, wo]
-    specs = [ANY] * n + ([] if first else [ANY]) + [smem, ANY, vmem] + [ANY] * 4
+    ins = list(us) + ([] if first else [z]) + [tok, w, wq, wk, wv, wo]
     alias = {} if first else {n: 0}
-    alias[len(specs) - 6] = 1
+    alias[len(ins) - 6] = 1
     pw = sum(range(QB, nt + 1, QB))
     return pl.pallas_call(
-        functools.partial(layer_kernel, first, n),
-        in_specs=specs,
+        functools.partial(layer_kernel, m, first, n),
+        in_specs=[ANY] * len(ins),
         out_specs=[ANY, ANY],
         out_shape=[jax.ShapeDtypeStruct((mb, 1, nt, d), BF16), TOK],
         input_output_aliases=alias,
         scratch_shapes=[pltpu.VMEM((nt, d), BF16)] * 3 + [pltpu.VMEM((nt, G * HD), BF16)] * 3 + [
             pltpu.VMEM((nt, d), BF16), pltpu.VMEM((G, QB, pw), F32), pltpu.VMEM((G, nt, HD), F32),
-            pltpu.VMEM((NR, d, G * HD), BF16), pltpu.SemaphoreType.DMA((NR,)),
-            pltpu.SemaphoreType.DMA((max(4, n),)), pltpu.SemaphoreType.DMA((ng,))],
+            pltpu.VMEM((NR, d, G * HD), BF16), pltpu.VMEM((1, d), F32), pltpu.SemaphoreType.DMA((NR,)),
+            pltpu.SemaphoreType.DMA((max(4, n),)), pltpu.SemaphoreType.DMA((ng,)), pltpu.SemaphoreType.DMA],
         compiler_params=pltpu.CompilerParams(vmem_limit_bytes=VMEM_LIMIT),
         cost_estimate=cost(8 * nt * d * d + 4 * nt * nt * d),
         name="layer",
@@ -523,9 +528,16 @@
             over_cap = (need > CAP).astype(jnp.int32).max().reshape(1)
             for axis, pairs in (('ep', peer), ('pp', over), ('ep', sibling)):
                 over_cap = jnp.maximum(over_cap, lax.ppermute(over_cap, axis, pairs))
-            st = jnp.concatenate([starts.reshape(-1), jnp.broadcast_to(over_cap, (128,))])
+            flags = jnp.broadcast_to(over_cap, (mb, 128 - starts[0].size))
+            st = jnp.concatenate([starts.reshape(mb, -1), flags], axis=1).reshape(-1)
             near, far, packed, rest, ys = {}, {}, {}, {}, {}
             z = None
+
+            def send_far(i, tok):
+                v, tok = lax.optimization_barrier((packed.pop(i), tok))
+                far[i] = lax.ppermute(v, 'ep', peer)
+                return tok
+
             for kind, m, e in order(mb):
                 if kind == 's':
                     s, tok = slice_rows(send, tok, o, m, e - m, cg)
@@ -536,7 +548,7 @@
                     v, tok = lax.optimization_barrier((wqkv[m], tok))
                     wqkv[m], tok = lax.optimization_barrier((jnp.reshape(v, (d, d)), tok))
                 elif kind in 'pb':
-                    jobs = [(i, w_, 0, CAP if w_ == FAR else full) for i in range(m, e) for w_ in (FAR, NEAR)]
+                    jobs = [(i, w_, 0, CAP) for i in range(m, e) for w_ in (FAR, NEAR)]
                     jobs = [b for b in jobs if (b[1] == FAR) == (kind == 'p') or b[0] > 0]
                     *out, tok = pack(tok, o, sib, tabs, jobs, cg)
                     for b, r in zip(jobs, out):
@@ -547,23 +559,25 @@
                         else:
                             packed[b[0]] = r
                 elif kind == 'e':
-                    def past(tok):
-                        *out, tok = pack(tok, o, sib, tabs, [(i, FAR, CAP, full - CAP) for i in range(m, e)], cg)
-                        return [lax.ppermute(v, 'ep', peer) for v in out] + [tok]
+                    def more(tok):
+                        past = [(i, w_, CAP, full - CAP) for w_ in (FAR, NEAR) for i in range(m, e)]
+                        *out, tok = pack(tok, o, sib, tabs, past, cg)
+                        return [lax.ppermute(v, 'ep', peer) for v in out[:e - m]] + out[e - m:] + [tok]
 
                     def none(tok):
-                        return list(nothing(tok, [(full - CAP, d)] * (e - m)))
-
-                    *out, tok = lax.cond(over_cap[0] > 0, past, none, tok)
-                    rest.update(zip(range(m, e), out))
-                    for i in sorted(packed):
-                        v, tok = lax.optimization_barrier((packed.pop(i), tok))
-                        far[i] = lax.ppermute(v, 'ep', peer)
+                        return list(nothing(tok, [(full - CAP, d)] * (2 * (e - m))))
+
+                    *out, tok = lax.cond(over_cap[0] > 0, more, none, tok)
+                    rest.update({i: (out[e - m + k], out[k]) for k, i in enumerate(range(m, e))})
+                    for i in sorted(packed)[:2]:
+                        tok = send_far(i, tok)
                 elif kind == 'c':
-                    y, tok = combine(st, tok, h, near[m], far[m], rest[m], cols, m)
+                    y, tok = combine(st, tok, h, near[m], far[m], *rest[m], cols, m, full)
                     ys[m] = [lax.ppermute(y, 'pp', over)]
                 else:
                     z, tok = layer(ys[m], z, m, tok, w, *wqkv, wo, mb)
+                    if m + 4 in packed:
+                        tok = send_far(m + 4, tok)
             return z
 
         return run(tok, {0: (d0, 0)})[None]

time: 1540 us -> 1330 us (0.86)
  waiting for transfers between devices: 495 us -> 296 us
    ppermute x7, waiting for transfers between devices: 414 us -> 215 us  [send_far(): far[i] = lax.ppermute(v, 'ep', peer)]
    unnamed x11 -> x12, local copies, waits for them, and re-layouts: 68.5 us -> 68.5 us
  transfers between devices with their start and end apart: 23 -> 23, of which waited for: 8 -> 7; matrix products, arithmetic and copies ran while one was open for 6% -> 6% of each run, Pallas kernels for 46% -> 53%
where the time goes in v1:
time: 1330 us; the launch traced here: 1320 us
  Pallas kernels  909 us (68%)
  waiting for transfers between devices  296 us (22%)
  local copies, waits for them, and re-layouts  73.1 us (5%)
  starting transfers between devices  29.9 us (2%)
    pallas_call x8, Pallas kernels, layer(): pl.pallas_call(functools.partial(layer_kernel, m, first, n), in_specs=[AN...  705 us
    ppermute x7, waiting for transfers between devices, send_far(): far[i] = lax.ppermute(v, 'ep', peer)  215 us
    pallas_call x8, Pallas kernels, combine(): pl.pallas_call(functools.partial(combine_kernel, m, full), in_specs=[ANY]...  86.4 us
    pallas_call x4, Pallas kernels, pack(): pl.pallas_call(functools.partial(pack_kernel, full, ne, cg, cap // cg, n)...  82.6 us
    ppermute x1, waiting for transfers between devices, run(): far[0] = lax.ppermute(r, 'ep', peer)  76.7 us
    unnamed x12, local copies, waits for them, and re-layouts  68.5 us
    pallas_call x3, Pallas kernels, slice_rows(): pl.pallas_call(slice_kernel, grid_spec=pltpu.PrefetchScalarGridSpec(num_s...  34.8 us
  transfers between devices with their start and end apart: 23, of which 7 were waited for; matrix products, arithmetic and copies ran while one was open for 6% of the time, Pallas kernels for 53%

profile of v1, /device:TPU:0, one launch (start us, length us, event | category | flops | bytes accessed | tf_op | source)
XLA Modules:
  0.0 1324.6 jit_solution(14873339119648587980)
XLA Ops:
  0.0 0.7 pad_add_fusion.1.rows_ref
  0.7 5.1 slice_rows.3
  5.8 0.8 collective-permute-start.11
  7.1 0.4 fusion.19
  7.5 0.4 copy.121
  8.9 2.3 reduce-window.14
  11.6 2.3 reduce-window.16
  14.8 5.4 select_reduce_fusion
  20.2 2.5 collective-permute-start.12
  22.7 1.8 collective-permute-done.12.refs_4_.refs_5_
  24.5 7.4 pack.8
  31.9 4.9 slice_rows.4
  36.9 0.6 fusion.23
  37.5 2.0 collective-permute-start.8
  39.5 1.9 collective-permute-done.8
  42.6 3.3 collective-permute-start.9
  45.9 0.4 collective-permute-done.9
  46.9 1.0 collective-permute-start.10
  47.9 0.3 collective-permute-done.10
  48.9 22.7 %copy.148 = bf16[512,8,32,128]{3,1,2,0:T(8,128)(2,1)} copy(bf16[512,8,32,128]{3,2,1,0:T(8,128)(2,1)} %bitcast.113) | data formatting | bytes 67108864
  71.5 16.3 %pack.9 = (bf16[576,4096]{1,0:T(8,128)(2,1)}, bf16[576,4096]{1,0:T(8,128)(2,1)}, bf16[576,4096]{1,0:T(8,128)(2,1)}, f32[8,128]{1,0:T(8,128)S(1)}) custom-call(f32[8,128]{1,0:T(8,128)S(1)} %get-tuple-element.165.refs_0_, bf16[8,2,640,4096]{3,2,1,0:T(8,128)(2,1)} %bitcast.17.o_ref.refs_1_, ...), custom_call_target="tpu_custom_call", output_to_operand_aliasing={{3}: (0, {})} | custom-call | flops 9059696640 | bytes 35389440 | tf_op jit(solution)/shard_map/pack/pallas_call | solution.py:128
  87.9 24.8 %slice_rows.5 = (bf16[6,2,2,160,4096]{4,3,2,1,0:T(8,128)(2,1)}, f32[8,128]{1,0:T(8,128)S(1)}) custom-call(s32[2]{0:T(128)} %pad_add_fusion.1.rows_ref, f32[8,128]{1,0:T(8,128)S(1)} %get-tuple-element.170.tok, bf16[8,2,640,4096]{3,2,1,0:T(8,128)(2,1)} %bitcast.17.o_ref.refs_1_), custom_call_target="tpu_custom_call", output_to_operand_aliasing={{1}: (1, {})} | custom-call | flops 12000000000 | bytes 46875000 | tf_op jit(solution)/shard_map/slice_rows/pallas_call | solution.py:32
  112.8 2.0 collective-permute-start.14
  116.7 0.8 stack.39.tab
  117.5 0.6 pad_bitcast_fusion.starts
  118.1 22.6 %copy.147 = bf16[512,8,32,128]{3,1,2,0:T(8,128)(2,1)} copy(bf16[512,8,32,128]{3,2,1,0:T(8,128)(2,1)} %bitcast.114) | data formatting | bytes 67108864
  140.7 76.7 %collective-permute-done.14.far = bf16[576,4096]{1,0:T(8,128)(2,1)} collective-permute-done((bf16[576,4096]{1,0:T(8,128)(2,1)}, bf16[576,4096]{1,0:T(8,128)(2,1)}, u32[]{:S(2)}, u32[]{:S(2)}) %collective-permute-start.14) | collective-permute-done | bytes 4718624 | tf_op jit(solution)/shard_map/ppermute | solution.py:558
  217.4 10.8 combine.8
  228.3 22.7 %copy.146 = bf16[512,8,32,128]{3,1,2,0:T(8,128)(2,1)} copy(bf16[512,8,32,128]{3,2,1,0:T(8,128)(2,1)} %bitcast.115) | data formatting | bytes 67108864
  251.0 29.5 %pack.10 = (bf16[576,4096]{1,0:T(8,128)(2,1)}, bf16[576,4096]{1,0:T(8,128)(2,1)}, bf16[576,4096]{1,0:T(8,128)(2,1)}, bf16[576,4096]{1,0:T(8,128)(2,1)}, bf16[576...) custom-call(f32[8,128]{1,0:T(8,128)S(1)} %get-tuple-element.182.refs_0_, ...), custom_call_target="tpu_custom_call", output_to_operand_aliasing={{6}: (0, {})} | custom-call | flops 18119393280 | bytes 70778880 | tf_op jit(solution)/shard_map/pack/pallas_call | solution.py:128
  280.4 29.4 %pack.11 = (bf16[576,4096]{1,0:T(8,128)(2,1)}, bf16[576,4096]{1,0:T(8,128)(2,1)}, bf16[576,4096]{1,0:T(8,128)(2,1)}, bf16[576,4096]{1,0:T(8,128)(2,1)}, bf16[576...) custom-call(f32[8,128]{1,0:T(8,128)S(1)} %get-tuple-element.184.refs_0_, ...), custom_call_target="tpu_custom_call", output_to_operand_aliasing={{6}: (0, {})} | custom-call | flops 18119393280 | bytes 70778880 | tf_op jit(solution)/shard_map/pack/pallas_call | solution.py:128
  309.9 0.4 conditional.3
  310.3 1.8 collective-permute-start.16
  312.1 1.5 collective-permute-start.18
  313.6 100.5 %collective-permute-done.16.far = bf16[576,4096]{1,0:T(8,128)(2,1)} collective-permute-done((bf16[576,4096]{1,0:T(8,128)(2,1)}, bf16[576,4096]{1,0:T(8,128)(2,1)}, u32[]{:S(2)}, u32[]{:S(2)}) %collective-permute-start.16) | collective-permute-done | bytes 4718624 | tf_op jit(solution)/shard_map/ppermute | solution.py:538
  414.1 10.7 combine.9
  424.8 1.6 collective-permute-start.17
  426.4 1.5 collective-permute-start.20
  427.8 0.5 collective-permute-start.19
  428.4 88.1 %layer.8 = (bf16[8,1,512,4096]{3,2,1,0:T(8,128)(2,1)}, f32[8,128]{1,0:T(8,128)S(1)}) custom-call(bf16[512,4096]{1,0:T(8,128)(2,1)} %collective-permute-done.18.refs_0_, f32[8,128]{1,0:T(8,128)S(1)} %get-tuple-element.199.refs_1_, f32[1,4096]{1,0:T(1,128)} %refs_3_.13, bf16[4096,4096]{1,0:T(8,128)(2,1)} %bitcast.116, ...), custom_call_target="tpu_custom_call", output_to_operand_aliasing={{1}: (1, {})} | custom-call | flops 73014444032 | bytes 285212672 | tf_op jit(solution)/shard_map/layer/pallas_call | solution.py:446
  516.5 1.5 collective-permute-start.23
  518.0 114.5 %collective-permute-done.19.far = bf16[576,4096]{1,0:T(8,128)(2,1)} collective-permute-done((bf16[576,4096]{1,0:T(8,128)(2,1)}, bf16[576,4096]{1,0:T(8,128)(2,1)}, u32[]{:S(2)}, u32[]{:S(2)}) %collective-permute-start.19) | collective-permute-done | bytes 4718624 | tf_op jit(solution)/shard_map/ppermute | solution.py:538
  632.5 10.8 combine.10
  643.3 0.5 collective-permute-start.22
  643.8 88.1 %layer.9 = (bf16[8,1,512,4096]{3,2,1,0:T(8,128)(2,1)}, f32[8,128]{1,0:T(8,128)S(1)}) custom-call(bf16[512,4096]{1,0:T(8,128)(2,1)} %collective-permute-done.17.refs_0_, bf16[8,1,512,4096]{3,2,1,0:T(8,128)(2,1)} %get-tuple-element.203.refs_1_, f32[8,128]{1,0:T(8,128)S(1)} %get-tuple-element.211.refs_2_, ...), custom_call_target="tpu_custom_call", output_to_operand_aliasing={{0}: (1, {}), {1}: (2, {})} | custom-call | flops 73014444032 | bytes 285212672 | tf_op jit(solution)/shard_map/layer/pallas_call | solution.py:446
  731.9 10.9 combine.11
  742.8 1.6 collective-permute-start.21
  744.4 1.5 collective-permute-start.24
  745.9 88.1 %layer.10 = (bf16[8,1,512,4096]{3,2,1,0:T(8,128)(2,1)}, f32[8,128]{1,0:T(8,128)S(1)}) custom-call(bf16[512,4096]{1,0:T(8,128)(2,1)} %collective-permute-done.22.refs_0_, bf16[8,1,512,4096]{3,2,1,0:T(8,128)(2,1)} %get-tuple-element.220.refs_1_, f32[8,128]{1,0:T(8,128)S(1)} %get-tuple-element.221.refs_2_, ...), custom_call_target="tpu_custom_call", output_to_operand_aliasing={{0}: (1, {}), {1}: (2, {})} | custom-call | flops 73014444032 | bytes 285212672 | tf_op jit(solution)/shard_map/layer/pallas_call | solution.py:446
  834.0 0.6 collective-permute-start.27
  834.5 10.8 combine.12
  845.4 0.5 collective-permute-start.26
  845.9 88.1 %layer.11 = (bf16[8,1,512,4096]{3,2,1,0:T(8,128)(2,1)}, f32[8,128]{1,0:T(8,128)S(1)}) custom-call(bf16[512,4096]{1,0:T(8,128)(2,1)} %collective-permute-done.21.refs_0_, bf16[8,1,512,4096]{3,2,1,0:T(8,128)(2,1)} %get-tuple-element.222.refs_1_, f32[8,128]{1,0:T(8,128)S(1)} %get-tuple-element.230.refs_2_, ...), custom_call_target="tpu_custom_call", output_to_operand_aliasing={{0}: (1, {}), {1}: (2, {})} | custom-call | flops 73014444032 | bytes 285212672 | tf_op jit(solution)/shard_map/layer/pallas_call | solution.py:446
  934.0 1.5 collective-permute-start.28
  935.5 11.0 combine.13
  946.5 1.6 collective-permute-start.25
  948.1 88.1 %layer.12 = (bf16[8,1,512,4096]{3,2,1,0:T(8,128)(2,1)}, f32[8,128]{1,0:T(8,128)S(1)}) custom-call(bf16[512,4096]{1,0:T(8,128)(2,1)} %collective-permute-done.26.refs_0_, bf16[8,1,512,4096]{3,2,1,0:T(8,128)(2,1)} %get-tuple-element.239.refs_1_, f32[8,128]{1,0:T(8,128)S(1)} %get-tuple-element.240.refs_2_, ...), custom_call_target="tpu_custom_call", output_to_operand_aliasing={{0}: (1, {}), {1}: (2, {})} | custom-call | flops 73014444032 | bytes 285212672 | tf_op jit(solution)/shard_map/layer/pallas_call | solution.py:446
  1036.2 10.6 combine.14
  1046.8 0.5 collective-permute-start.30
  1047.3 88.1 %layer.13 = (bf16[8,1,512,4096]{3,2,1,0:T(8,128)(2,1)}, f32[8,128]{1,0:T(8,128)S(1)}) custom-call(bf16[512,4096]{1,0:T(8,128)(2,1)} %collective-permute-done.25.refs_0_, bf16[8,1,512,4096]{3,2,1,0:T(8,128)(2,1)} %get-tuple-element.241.refs_1_, f32[8,128]{1,0:T(8,128)S(1)} %get-tuple-element.247.refs_2_, ...), custom_call_target="tpu_custom_call", output_to_operand_aliasing={{0}: (1, {}), {1}: (2, {})} | custom-call | flops 73014444032 | bytes 285212672 | tf_op jit(solution)/shard_map/layer/pallas_call | solution.py:446
  1135.4 10.7 combine.15
  1146.2 1.5 collective-permute-start.29
  1147.7 88.1 %layer.14 = (bf16[8,1,512,4096]{3,2,1,0:T(8,128)(2,1)}, f32[8,128]{1,0:T(8,128)S(1)}) custom-call(bf16[512,4096]{1,0:T(8,128)(2,1)} %collective-permute-done.30.refs_0_, bf16[8,1,512,4096]{3,2,1,0:T(8,128)(2,1)} %get-tuple-element.255.refs_1_, f32[8,128]{1,0:T(8,128)S(1)} %get-tuple-element.256.refs_2_, ...), custom_call_target="tpu_custom_call", output_to_operand_aliasing={{0}: (1, {}), {1}: (2, {})} | custom-call | flops 73014444032 | bytes 285212672 | tf_op jit(solution)/shard_map/layer/pallas_call | solution.py:446
  1235.8 88.3 %layer.15 = (bf16[8,1,512,4096]{3,2,1,0:T(8,128)(2,1)}, f32[8,128]{1,0:T(8,128)S(1)}) custom-call(bf16[512,4096]{1,0:T(8,128)(2,1)} %collective-permute-done.29.refs_0_, bf16[8,1,512,4096]{3,2,1,0:T(8,128)(2,1)} %get-tuple-element.257.refs_1_, f32[8,128]{1,0:T(8,128)S(1)} %get-tuple-element.258.refs_2_, ...), custom_call_target="tpu_custom_call", output_to_operand_aliasing={{0}: (1, {}), {1}: (2, {})} | custom-call | flops 73014444032 | bytes 285212672 | tf_op jit(solution)/shard_map/layer/pallas_call | solution.py:446
  (69 shorter events, 4.7 us)
Async XLA Ops:
  0.7 5.9 copy-start
  0.7 6.2 copy-start.1
  5.8 18.7 %collective-permute-start.11 = (bf16[1,2,2,160,4096]{4,3,2,1,0:T(8,128)(2,1)}, bf16[1,2,2,160,4096]{4,3,2,1,0:T(8,128)(2,1)}, u32[]{:S(2)}, u32[]{:S(2)}) collective-permute-start(bf16[1,2,2,160,4096]{4,3,2,1,0:T(8,128)(2,1)} %get-tuple-element.160), channel_id=1, source_target_pairs={{0,1},{1,0},{2,3},{3,2},{4,5},{5,4},{6,7},{7,6}} | collective-permute-start | bytes 15728648 | tf_op jit(solution)/shard_map/ppermute | solution.py:524
  20.2 4.3 collective-permute-start.12
  36.9 34.6 %collective-permute-start.13 = (bf16[1,2,2,160,4096]{4,3,2,1,0:T(8,128)(2,1)}, bf16[1,2,2,160,4096]{4,3,2,1,0:T(8,128)(2,1)}, u32[]{:S(2)}, u32[]{:S(2)}) collective-permute-start(bf16[1,2,2,160,4096]{4,3,2,1,0:T(8,128)(2,1)} %get-tuple-element.166), channel_id=1, source_target_pairs={{0,1},{1,0},{2,3},{3,2},{4,5},{5,4},{6,7},{7,6}} | collective-permute-start | bytes 15728648 | tf_op jit(solution)/shard_map/ppermute | solution.py:544
  37.5 3.9 collective-permute-start.8
  42.6 3.7 collective-permute-start.9
  46.9 1.3 collective-permute-start.10
  87.8 28.8 %copy-start.2 = (f32[1,8,1,512,2]{3,4,2,1,0:T(2,128)S(1)}, f32[1,8,1,512,2]{3,4,2,1,0:T(2,128)}, u32[]{:S(2)}) copy-start(f32[1,8,1,512,2]{3,4,2,1,0:T(2,128)} %param.17) | copy-start | bytes 98308
  112.7 138.3 %collective-permute-start.15 = (bf16[6,2,2,160,4096]{4,3,2,1,0:T(8,128)(2,1)}, bf16[6,2,2,160,4096]{4,3,2,1,0:T(8,128)(2,1)}, u32[]{:S(2)}, u32[]{:S(2)}) collective-permute-start(bf16[6,2,2,160,4096]{4,3,2,1,0:T(8,128)(2,1)} %get-tuple-element.183), channel_id=1, source_target_pairs={{0,1},{1,0},{2,3},{3,2},{4,5},{5,4},{6,7},{7,6}} | collective-permute-start | bytes 94371848 | tf_op jit(solution)/shard_map/ppermute | solution.py:544
  112.8 104.6 %collective-permute-start.14 = (bf16[576,4096]{1,0:T(8,128)(2,1)}, bf16[576,4096]{1,0:T(8,128)(2,1)}, u32[]{:S(2)}, u32[]{:S(2)}) collective-permute-start(bf16[576,4096]{1,0:T(8,128)(2,1)} %get-tuple-element.176), channel_id=1, source_target_pairs={{0,2},{1,3},{2,0},{3,1},{4,6},{5,7},{6,4},{7,5}} | collective-permute-start | bytes 14155784 | tf_op jit(solution)/shard_map/ppermute | solution.py:558
  310.3 103.8 %collective-permute-start.16 = (bf16[576,4096]{1,0:T(8,128)(2,1)}, bf16[576,4096]{1,0:T(8,128)(2,1)}, u32[]{:S(2)}, u32[]{:S(2)}) collective-permute-start(bf16[576,4096]{1,0:T(8,128)(2,1)} %get-tuple-element.194), channel_id=1, source_target_pairs={{0,2},{1,3},{2,0},{3,1},{4,6},{5,7},{6,4},{7,5}} | collective-permute-start | bytes 14155784 | tf_op jit(solution)/shard_map/ppermute | solution.py:538
  312.1 116.3 %collective-permute-start.18 = (bf16[512,4096]{1,0:T(8,128)(2,1)}, bf16[512,4096]{1,0:T(8,128)(2,1)}, u32[]{:S(2)}, u32[]{:S(2)}) collective-permute-start(bf16[512,4096]{1,0:T(8,128)(2,1)} %get-tuple-element.198), channel_id=1, source_target_pairs={{0,4},{4,0},{1,5},{5,1},{2,6},{6,2},{3,7},{7,3}} | collective-permute-start | bytes 12582920 | tf_op jit(solution)/shard_map/ppermute | solution.py:576
  424.8 219.0 %collective-permute-start.17 = (bf16[512,4096]{1,0:T(8,128)(2,1)}, bf16[512,4096]{1,0:T(8,128)(2,1)}, u32[]{:S(2)}, u32[]{:S(2)}) collective-permute-start(bf16[512,4096]{1,0:T(8,128)(2,1)} %get-tuple-element.197), channel_id=1, source_target_pairs={{0,4},{4,0},{1,5},{5,1},{2,6},{6,2},{3,7},{7,3}} | collective-permute-start | bytes 12582920 | tf_op jit(solution)/shard_map/ppermute | solution.py:576
  426.4 305.5 %collective-permute-start.20 = (bf16[576,4096]{1,0:T(8,128)(2,1)}, bf16[576,4096]{1,0:T(8,128)(2,1)}, u32[]{:S(2)}, u32[]{:S(2)}) collective-permute-start(bf16[576,4096]{1,0:T(8,128)(2,1)} %get-tuple-element.215), channel_id=1, source_target_pairs={{0,2},{1,3},{2,0},{3,1},{4,6},{5,7},{6,4},{7,5}} | collective-permute-start | bytes 14155784 | tf_op jit(solution)/shard_map/ppermute | solution.py:538
  427.8 204.6 %collective-permute-start.19 = (bf16[576,4096]{1,0:T(8,128)(2,1)}, bf16[576,4096]{1,0:T(8,128)(2,1)}, u32[]{:S(2)}, u32[]{:S(2)}) collective-permute-start(bf16[576,4096]{1,0:T(8,128)(2,1)} %get-tuple-element.208), channel_id=1, source_target_pairs={{0,2},{1,3},{2,0},{3,1},{4,6},{5,7},{6,4},{7,5}} | collective-permute-start | bytes 14155784 | tf_op jit(solution)/shard_map/ppermute | solution.py:538
  516.5 318.0 %collective-permute-start.23 = (bf16[576,4096]{1,0:T(8,128)(2,1)}, bf16[576,4096]{1,0:T(8,128)(2,1)}, u32[]{:S(2)}, u32[]{:S(2)}) collective-permute-start(bf16[576,4096]{1,0:T(8,128)(2,1)} %get-tuple-element.227), channel_id=1, source_target_pairs={{0,2},{1,3},{2,0},{3,1},{4,6},{5,7},{6,4},{7,5}} | collective-permute-start | bytes 14155784 | tf_op jit(solution)/shard_map/ppermute | solution.py:538
  643.3 102.6 %collective-permute-start.22 = (bf16[512,4096]{1,0:T(8,128)(2,1)}, bf16[512,4096]{1,0:T(8,128)(2,1)}, u32[]{:S(2)}, u32[]{:S(2)}) collective-permute-start(bf16[512,4096]{1,0:T(8,128)(2,1)} %get-tuple-element.219), channel_id=1, source_target_pairs={{0,4},{4,0},{1,5},{5,1},{2,6},{6,2},{3,7},{7,3}} | collective-permute-start | bytes 12582920 | tf_op jit(solution)/shard_map/ppermute | solution.py:576
  742.8 103.1 %collective-permute-start.21 = (bf16[512,4096]{1,0:T(8,128)(2,1)}, bf16[512,4096]{1,0:T(8,128)(2,1)}, u32[]{:S(2)}, u32[]{:S(2)}) collective-permute-start(bf16[512,4096]{1,0:T(8,128)(2,1)} %get-tuple-element.218), channel_id=1, source_target_pairs={{0,4},{4,0},{1,5},{5,1},{2,6},{6,2},{3,7},{7,3}} | collective-permute-start | bytes 12582920 | tf_op jit(solution)/shard_map/ppermute | solution.py:576
  744.4 191.1 %collective-permute-start.24 = (bf16[576,4096]{1,0:T(8,128)(2,1)}, bf16[576,4096]{1,0:T(8,128)(2,1)}, u32[]{:S(2)}, u32[]{:S(2)}) collective-permute-start(bf16[576,4096]{1,0:T(8,128)(2,1)} %get-tuple-element.234), channel_id=1, source_target_pairs={{0,2},{1,3},{2,0},{3,1},{4,6},{5,7},{6,4},{7,5}} | collective-permute-start | bytes 14155784 | tf_op jit(solution)/shard_map/ppermute | solution.py:538
  834.0 202.2 %collective-permute-start.27 = (bf16[576,4096]{1,0:T(8,128)(2,1)}, bf16[576,4096]{1,0:T(8,128)(2,1)}, u32[]{:S(2)}, u32[]{:S(2)}) collective-permute-start(bf16[576,4096]{1,0:T(8,128)(2,1)} %get-tuple-element.244), channel_id=1, source_target_pairs={{0,2},{1,3},{2,0},{3,1},{4,6},{5,7},{6,4},{7,5}} | collective-permute-start | bytes 14155784 | tf_op jit(solution)/shard_map/ppermute | solution.py:538
  845.4 102.7 %collective-permute-start.26 = (bf16[512,4096]{1,0:T(8,128)(2,1)}, bf16[512,4096]{1,0:T(8,128)(2,1)}, u32[]{:S(2)}, u32[]{:S(2)}) collective-permute-start(bf16[512,4096]{1,0:T(8,128)(2,1)} %get-tuple-element.238), channel_id=1, source_target_pairs={{0,4},{4,0},{1,5},{5,1},{2,6},{6,2},{3,7},{7,3}} | collective-permute-start | bytes 12582920 | tf_op jit(solution)/shard_map/ppermute | solution.py:576
  934.0 201.5 %collective-permute-start.28 = (bf16[576,4096]{1,0:T(8,128)(2,1)}, bf16[576,4096]{1,0:T(8,128)(2,1)}, u32[]{:S(2)}, u32[]{:S(2)}) collective-permute-start(bf16[576,4096]{1,0:T(8,128)(2,1)} %get-tuple-element.250), channel_id=1, source_target_pairs={{0,2},{1,3},{2,0},{3,1},{4,6},{5,7},{6,4},{7,5}} | collective-permute-start | bytes 14155784 | tf_op jit(solution)/shard_map/ppermute | solution.py:538
  946.5 100.8 %collective-permute-start.25 = (bf16[512,4096]{1,0:T(8,128)(2,1)}, bf16[512,4096]{1,0:T(8,128)(2,1)}, u32[]{:S(2)}, u32[]{:S(2)}) collective-permute-start(bf16[512,4096]{1,0:T(8,128)(2,1)} %get-tuple-element.237), channel_id=1, source_target_pairs={{0,4},{4,0},{1,5},{5,1},{2,6},{6,2},{3,7},{7,3}} | collective-permute-start | bytes 12582920 | tf_op jit(solution)/shard_map/ppermute | solution.py:576
  1046.8 100.9 %collective-permute-start.30 = (bf16[512,4096]{1,0:T(8,128)(2,1)}, bf16[512,4096]{1,0:T(8,128)(2,1)}, u32[]{:S(2)}, u32[]{:S(2)}) collective-permute-start(bf16[512,4096]{1,0:T(8,128)(2,1)} %get-tuple-element.254), channel_id=1, source_target_pairs={{0,4},{4,0},{1,5},{5,1},{2,6},{6,2},{3,7},{7,3}} | collective-permute-start | bytes 12582920 | tf_op jit(solution)/shard_map/ppermute | solution.py:576
  1146.2 89.6 %collective-permute-start.29 = (bf16[512,4096]{1,0:T(8,128)(2,1)}, bf16[512,4096]{1,0:T(8,128)(2,1)}, u32[]{:S(2)}, u32[]{:S(2)}) collective-permute-start(bf16[512,4096]{1,0:T(8,128)(2,1)} %get-tuple-element.253), channel_id=1, source_target_pairs={{0,4},{4,0},{1,5},{5,1},{2,6},{6,2},{3,7},{7,3}} | collective-permute-start | bytes 12582920 | tf_op jit(solution)/shard_map/ppermute | solution.py:576
